TPU v7x, 32 devices: a whole 2x2x4 slice. The times are simulated.
32 devices in a mesh: grp: 16 (over z, y, x), rep: 2 (over core).
Axes of the slice: x: 2, y: 2, z: 4, core: 2. Of those that a mesh axis runs over, the one named last changes fastest.
Arguments:
- vectors: bfloat16 [4096, 768], P(('grp', 'rep')), may hold values from -6 to 6
- list_ids: int32 [4096, 8], P(('grp', 'rep')), may hold values from -1 to 8191, as said below
- spill_weight: int32 [4096, 8], P(('grp', 'rep')), may hold values from 1 to 4
- list_pos: int32 [8192], replicated, may hold values from 0 to 8191, as said below
- old_centroids: float32 [8192, 768], P('grp'), may hold values from -12 to 12
Outputs:
- refined: float32 [8192, 768], P('grp')
- new_dist: float32 [4096, 8], P(('grp', 'rep'))
Inputs may be any that keep to these rules, and one draw needn't show every extreme that they name: `list_ids`: entries are list numbers or -1; the lists of one row are distinct. List l is owned by grp index list_pos[l] // 512. Among the rows of one device (aligned blocks of 128 rows), at most 32 slots name lists of one owner, and in every block some owner gets exactly 32. `list_pos`: A permutation of the list numbers.
All inputs are finite; a program needn't handle non-finite values.
Results may differ from a plain program's by a relative error of at most 0.0003.
Values may be sent and summed in bfloat16 or wider, within the bound.
A program may use at most 64 MiB of HBM per device.

v0:
```python
import functools
import math

import jax
import jax.numpy as jnp
from jax import lax
from jax.experimental import pallas as pl
from jax.experimental.pallas import tpu as pltpu
from jax.sharding import PartitionSpec as P

D = 768


def decode_meta(meta_rows):
    values = meta_rows.astype(jnp.int32)
    tag_value = values[:, 0] * 128 + values[:, 1]
    return (tag_value > 0, jnp.maximum(tag_value - 1, 0), values[:, 2].astype(jnp.float32))


def pick_block(table, index_block):
    table_iota = jnp.arange(table.shape[0], dtype=jnp.int32)
    if table.dtype == jnp.float32:
        selector = (index_block[:, None] == table_iota[None, :]).astype(jnp.float32)
        return jnp.dot(
            selector, table, precision=lax.Precision.HIGHEST, preferred_element_type=jnp.float32
        )
    selector = (index_block[:, None] == table_iota[None, :]).astype(table.dtype)
    return jnp.dot(selector, table, preferred_element_type=jnp.float32).astype(table.dtype)


def pick_rows(table, indices):
    total_rows = indices.shape[0]
    block_rows = math.gcd(512, total_rows)
    block_count = total_rows // block_rows
    picked = lax.map(
        lambda index_block: pick_block(table, index_block), indices.reshape(block_count, block_rows)
    )
    return picked.reshape(total_rows, table.shape[1])


def owner_sums(rows_all, slot_all, weight_all, old_centroids, lists_here):
    total_rows, feature_dim = rows_all.shape
    block_rows = math.gcd(512, total_rows)
    block_count = total_rows // block_rows
    row_blocks = rows_all.reshape(block_count, block_rows, feature_dim)
    slot_blocks = slot_all.reshape(block_count, block_rows)
    weight_blocks = weight_all.reshape(block_count, block_rows)
    list_iota = jnp.arange(lists_here, dtype=jnp.int32)

    def accumulate(running, piece_item):
        weighted_sums, totals = running
        rows_in, slot_in, weight_in = piece_item
        row_values = rows_in.astype(jnp.float32)
        centre_rows = pick_block(old_centroids, slot_in)
        sq_norms = jnp.sum((row_values - centre_rows) ** 2, axis=-1)
        shares = weight_in / (1.0 + sq_norms / D)
        placed = (slot_in[None, :] == list_iota[:, None]).astype(jnp.float32) * shares[None, :]
        weighted_sums = weighted_sums + jnp.dot(
            placed, row_values, precision=lax.Precision.HIGHEST, preferred_element_type=jnp.float32
        )
        totals = totals + jnp.sum(placed, axis=1)
        return ((weighted_sums, totals), jnp.float32(0.0))

    start_state = (
        jnp.zeros((lists_here, feature_dim), jnp.float32),
        jnp.zeros((lists_here,), jnp.float32),
    )
    final_state, unused = lax.scan(
        accumulate, start_state, (row_blocks, slot_blocks, weight_blocks)
    )
    return final_state


def shards_general(vectors, list_ids, spill_weight, list_pos, old_centroids):
    owners = lax.axis_size("grp")
    row_count, slot_count = list_ids.shape
    feature_dim = vectors.shape[1]
    lists_here = old_centroids.shape[0]
    cap_slots = row_count * slot_count // (2 * owners)
    seat_total = owners * cap_slots
    pair_count = row_count * slot_count
    is_live = list_ids >= 0
    places = jnp.where(is_live, list_pos[jnp.maximum(list_ids, 0)], 0)
    target = jnp.where(is_live, places // lists_here, owners).reshape(-1)
    sorted_order = jnp.argsort(target, stable=True)
    ranked = target[sorted_order]
    counts = jnp.sum(
        (target[:, None] == jnp.arange(owners, dtype=jnp.int32)[None, :]).astype(jnp.int32), axis=0
    )
    starts = jnp.concatenate([jnp.cumsum(counts) - counts, jnp.zeros((1,), jnp.int32)])
    within = jnp.arange(pair_count, dtype=jnp.int32) - starts[ranked]
    seat_sorted = jnp.where(ranked < owners, ranked * cap_slots + within, seat_total)
    seat_index = jnp.zeros((pair_count,), jnp.int32).at[sorted_order].set(seat_sorted)
    pair_of_seat = (
        jnp.full((seat_total,), -1, jnp.int32)
        .at[seat_index]
        .set(jnp.arange(pair_count, dtype=jnp.int32), mode="drop")
    )
    filled = pair_of_seat >= 0
    pair_safe = jnp.maximum(pair_of_seat, 0)
    source_row = jnp.where(filled, pair_safe // slot_count, -1)
    send_rows = pick_rows(vectors, source_row)
    local_flat = (places % lists_here).reshape(-1)
    weight_flat = spill_weight.reshape(-1)
    tag_out = jnp.where(filled, local_flat[pair_safe] + 1, 0)
    weight_out = jnp.where(filled, weight_flat[pair_safe], 0)
    send_meta = jnp.stack([tag_out // 128, tag_out % 128, weight_out], axis=-1).astype(jnp.bfloat16)
    got_rows, got_meta = (
        lax.all_to_all(
            send_rows.reshape(owners, cap_slots, feature_dim),
            "grp",
            split_axis=0,
            concat_axis=0,
            tiled=True,
        ),
        lax.all_to_all(
            send_meta.reshape(owners, cap_slots, 3), "grp", split_axis=0, concat_axis=0, tiled=True
        ),
    )
    got_rows = got_rows.reshape(seat_total, feature_dim)
    got_meta = got_meta.reshape(seat_total, 3)
    seat_live, seat_row, seat_weight = decode_meta(got_meta)
    weighted_sums, totals = owner_sums(got_rows, seat_row, seat_weight, old_centroids, lists_here)
    weighted_sums, totals = lax.psum((weighted_sums, totals), "rep")
    refined = (old_centroids + weighted_sums) / (1.0 + totals[:, None])
    block_rows = math.gcd(512, seat_total)
    block_count = seat_total // block_rows
    row_blocks = got_rows.reshape(block_count, block_rows, feature_dim)
    slot_blocks = seat_row.reshape(block_count, block_rows)

    def distance(piece_item):
        rows_in, slot_in = piece_item
        row_values = rows_in.astype(jnp.float32)
        return jnp.sum((row_values - pick_block(refined, slot_in)) ** 2, axis=-1) / D

    owner_dist = lax.map(distance, (row_blocks, slot_blocks)).reshape(owners, cap_slots)
    seat_dist = lax.all_to_all(owner_dist, "grp", split_axis=0, concat_axis=0, tiled=True).reshape(
        seat_total
    )
    picked = seat_dist[jnp.minimum(seat_index, seat_total - 1)].reshape(row_count, slot_count)
    new_dist = jnp.where(is_live, picked, jnp.float32(0.0))
    return (refined, new_dist)


MESH = pl.DeviceIdType.MESH
LANES = 128
CHUNKS = 1
F32 = jnp.float32
BF16 = jnp.bfloat16


def xor_index(a, b_const, bits):
    out = 0
    for i in range(bits):
        bit = (a // (1 << i)) % 2
        out = out + ((1 - bit) if (b_const >> i) & 1 else bit) * (1 << i)
    return out


def split_two(x):
    hi = x.astype(BF16)
    return hi, (x - hi.astype(F32)).astype(BF16)


def dot(a, b):
    return jnp.dot(a, b, preferred_element_type=F32)


def iota(shape, dim):
    return lax.broadcasted_iota(jnp.int32, shape, dim)


def fused_kernel(
    owners, cap,
    vec_ref, ids_ref, weight_ref, pos_ref, cent_hbm,
    refined_ref, dist_ref,
    cent, cent_hi, cent_lo, send_buf, meta_send, rows, metas, sib_rows, sib_metas,
    acc, tot, back_send, back, seat_keep, send_up, up_rows, sib_up, raw_in, seat_out, seat_in, up_mask, up_placed,
    local_sem, s_raw, r_raw, s_seat, r_seat, s_up, r_up, s_fup, r_fup, s_rows, r_rows, s_meta, r_meta, s_fwd, r_fwd, s_fmeta, r_fmeta, s_back, r_back,
):
    me = lax.axis_index("grp")
    rep = lax.axis_index("rep")
    bits = owners.bit_length() - 1
    row_count, feature_dim = vec_ref.shape
    slot_count = ids_ref.shape[0]
    lists_here = cent.shape[0]
    groups = owners * cap // LANES
    per_group = owners // groups
    upper = owners // 2
    half_groups = groups // 2
    up_seats = upper * cap
    chunk = feature_dim // CHUNKS
    peers = [xor_index(me, j, bits) for j in range(owners)]

    barrier = pltpu.get_barrier_semaphore()
    for j in range(1, owners):
        pl.semaphore_signal(barrier, inc=1, device_id={"grp": peers[j]}, device_id_type=MESH)
    pl.semaphore_signal(barrier, inc=1, device_id={"rep": 1 - rep}, device_id_type=MESH)
    cent_copy = pltpu.make_async_copy(cent_hbm, cent, local_sem)
    cent_copy.start()

    def raw_copy(c):
        span = pl.ds(c * chunk, chunk)
        return pltpu.make_async_remote_copy(
            src_ref=vec_ref.at[:, span], dst_ref=raw_in.at[c], send_sem=s_raw.at[c],
            recv_sem=r_raw.at[c], device_id={"grp": peers[upper]}, device_id_type=MESH,
        )

    pl.semaphore_wait(barrier, owners)
    for c in range(CHUNKS):
        raw_copy(c).start()

    table = pos_ref[...]
    table_rows = table.shape[0]
    table_bytes = jnp.concatenate([table // 256, table % 256], axis=1).astype(F32).astype(BF16)
    ids = jnp.transpose(ids_ref[...])
    weights = jnp.transpose(weight_ref[...])
    lane = iota((row_count, LANES), 1)
    id_cols = [ids[:, k : k + 1] for k in range(slot_count)]
    hi_one = jnp.concatenate(
        [
            (iota((row_count, table_rows), 1) == jnp.maximum(c, 0) // LANES).astype(F32).astype(BF16)
            for c in id_cols
        ],
        axis=0,
    )
    looked = dot(hi_one, table_bytes)
    place_values = looked[:, :LANES] * 256.0 + looked[:, LANES:]
    live_cols, owner_cols, code_cols = [], [], []
    for k in range(slot_count):
        c = id_cols[k]
        part = place_values[k * row_count : (k + 1) * row_count]
        place = jnp.sum(
            jnp.where(lane == jnp.maximum(c, 0) % LANES, part, 0.0), axis=1, keepdims=True
        ).astype(jnp.int32)
        owner = place // lists_here
        live_cols.append(c >= 0)
        owner_cols.append(jnp.where(c >= 0, owner ^ me, -1))
        code_cols.append(((place % lists_here) * 8 + weights[:, k : k + 1]).astype(F32))

    member = [(lane == o) for o in owner_cols]
    ones = [m.astype(F32) for m in member]
    lower = (iota((row_count, row_count), 0) > iota((row_count, row_count), 1)).astype(F32).astype(BF16)
    before = dot(lower, jnp.concatenate(ones, axis=1).astype(BF16))
    base = jnp.zeros((1, LANES), F32)
    seats_lane = jnp.full((row_count, LANES), -1.0, F32)
    seat_cols = []
    for k in range(slot_count):
        inside = before[:, k * LANES : (k + 1) * LANES] + base
        rank = jnp.sum(jnp.where(member[k], inside, 0.0), axis=1, keepdims=True)
        base = base + jnp.sum(ones[k], axis=0, keepdims=True)
        seat = jnp.where(live_cols[k], owner_cols[k].astype(F32) * cap + rank, -1.0)
        seat_cols.append(seat)
        seats_lane = jnp.where(lane == k, seat, seats_lane)
    seat_keep[...] = seats_lane
    seat_rows = jnp.transpose(seats_lane)
    seat_out[...] = seat_rows[:slot_count]

    seat_copy = pltpu.make_async_remote_copy(
        src_ref=seat_out, dst_ref=seat_in, send_sem=s_seat, recv_sem=r_seat,
        device_id={"grp": peers[upper]}, device_id_type=MESH,
    )

    def relay_copy(c, j):
        return pltpu.make_async_remote_copy(
            src_ref=send_up.at[c, j], dst_ref=up_rows.at[c, j],
            send_sem=s_up.at[c, j], recv_sem=r_up.at[c, j],
            device_id={"grp": peers[j]}, device_id_type=MESH,
        )

    def forward_up(c, h):
        part = pl.ds(h * (upper // 2), upper // 2)
        return pltpu.make_async_remote_copy(
            src_ref=up_rows.at[c, part], dst_ref=sib_up.at[c, part],
            send_sem=s_fup.at[c, h], recv_sem=r_fup.at[c, h],
            device_id={"rep": 1 - rep}, device_id_type=MESH,
        )

    seat_copy.start()

    for g in range(groups):
        q = (lane + g * LANES).astype(F32)
        code = jnp.zeros((row_count, LANES), F32)
        for k in range(slot_count):
            code = code + jnp.where(seat_cols[k] == q, code_cols[k], 0.0)
        meta_send[g] = jnp.sum(code, axis=0, keepdims=True)

    vectors = vec_ref[...]

    def row_copy(j):
        return pltpu.make_async_remote_copy(
            src_ref=send_buf.at[j], dst_ref=rows.at[j], send_sem=s_rows.at[j], recv_sem=r_rows.at[j],
            device_id={"grp": peers[j]}, device_id_type=MESH,
        )

    def meta_copy(j):
        return pltpu.make_async_remote_copy(
            src_ref=meta_send.at[j // per_group], dst_ref=metas.at[j], send_sem=s_meta.at[j],
            recv_sem=r_meta.at[j], device_id={"grp": peers[j]}, device_id_type=MESH,
        )

    def back_copy(j):
        return pltpu.make_async_remote_copy(
            src_ref=back_send.at[j // per_group], dst_ref=back.at[j], send_sem=s_back.at[j],
            recv_sem=r_back.at[j], device_id={"grp": peers[j]}, device_id_type=MESH,
        )

    def forward_copy(g):
        span = pl.ds(g * per_group, per_group)
        return pltpu.make_async_remote_copy(
            src_ref=rows.at[span], dst_ref=sib_rows.at[span], send_sem=s_fwd.at[g], recv_sem=r_fwd.at[g],
            device_id={"rep": 1 - rep}, device_id_type=MESH,
        )

    def forward_meta(g):
        span = pl.ds(g * per_group, per_group)
        return pltpu.make_async_remote_copy(
            src_ref=metas.at[span], dst_ref=sib_metas.at[span], send_sem=s_fmeta.at[g],
            recv_sem=r_fmeta.at[g], device_id={"rep": 1 - rep}, device_id_type=MESH,
        )

    for j in reversed(range(1, owners)):
        meta_copy(j).start()
    metas[0] = meta_send[0]

    def pick_rows_of(seat_table, first, count, values):
        q = (iota((count, row_count), 0) + first).astype(F32)
        pick = jnp.zeros((count, row_count), F32)
        for k in range(slot_count):
            pick = pick + (seat_table[k : k + 1, :] == q).astype(F32)
        pick = pick.astype(BF16)
        return pick if values is None else dot(pick, values).astype(BF16)

    picked = pick_rows_of(seat_rows, 0, up_seats, vectors).reshape(upper, cap, feature_dim)
    send_buf[pl.ds(0, upper)] = picked
    rows[0] = picked[0]
    for j in reversed(range(1, upper)):
        row_copy(j).start()

    cent_copy.wait()
    hi, lo = split_two(cent[...])
    cent_hi[...] = hi
    cent_lo[...] = lo
    acc[...] = cent[...]
    tot[...] = jnp.zeros_like(tot)

    lane_row = iota((1, LANES), 1)

    def meta_row(ref, g):
        out = ref[g * per_group]
        for b in range(1, per_group):
            out = jnp.where(lane_row // cap == b, ref[g * per_group + b], out)
        return out

    def codes_of(own, g):
        row = meta_row(metas if own else sib_metas, g).astype(jnp.int32)
        col = jnp.transpose(jnp.broadcast_to(row, (LANES, LANES)))
        return row, col

    def gather_mask(col):
        wide = jnp.concatenate([col // 8] * (lists_here // LANES), axis=1)
        return (wide == iota((LANES, lists_here), 1)).astype(F32).astype(BF16)

    def shares_of(weight, sq):
        share = weight / (1.0 + sq / feature_dim)
        count = share.shape[0]
        hi_part = share.astype(BF16).astype(F32)
        at = iota((count, LANES), 1)
        two = jnp.where(at == 0, hi_part, jnp.where(at == 1, share - hi_part, 0.0))
        return share, two.astype(BF16)

    def lower_group(g):
        for j in range(max(g * per_group, 1), (g + 1) * per_group):
            meta_copy(j).wait_recv()
            row_copy(j).wait_recv()
        forward_meta(g).start()
        forward_copy(g).start()
        row_a, col_a = codes_of(True, g)
        mask_a = gather_mask(col_a)
        span = pl.ds(g * per_group, per_group)
        forward_meta(g).wait_recv()
        row_b, col_b = codes_of(False, g)
        mask_b = gather_mask(col_b)
        mask = jnp.concatenate([mask_a, mask_b], axis=0)
        centre = dot(mask, cent_hi[...]) + dot(mask, cent_lo[...])
        forward_copy(g).wait_recv()
        got = jnp.concatenate(
            [rows[span].reshape(LANES, feature_dim), sib_rows[span].reshape(LANES, feature_dim)], axis=0
        ).astype(F32)
        weight = jnp.concatenate([col_a[:, :1] % 8, col_b[:, :1] % 8], axis=0).astype(F32)
        diff = got - centre
        share, share_two = shares_of(weight, jnp.sum(diff * diff, axis=1, keepdims=True))
        sv_hi, sv_lo = split_two(share * got)
        both = jnp.concatenate([row_a, row_b], axis=1) // 8
        placed = (both == iota((lists_here, 2 * LANES), 0)).astype(F32).astype(BF16)
        acc[...] += dot(placed, sv_hi) + dot(placed, sv_lo)
        tot[...] += dot(placed, share_two)

    seat_copy.wait_recv()
    mirror_pick = pick_rows_of(seat_in[...], up_seats, up_seats, None)

    def relay(c):
        raw_copy(c).wait_recv()
        part = dot(mirror_pick, raw_in[c]).astype(BF16).reshape(upper, cap, chunk)
        send_up[c] = part
        up_rows[c, 0] = part[0]
        for j in reversed(range(1, upper)):
            relay_copy(c, j).start()

    up_weights = []

    def upper_codes():
        for g in range(half_groups, groups):
            for j in range(g * per_group, (g + 1) * per_group):
                meta_copy(j).wait_recv()
            forward_meta(g).start()
        for own in (True, False):
            for g in range(half_groups, groups):
                if not own:
                    forward_meta(g).wait_recv()
                row, col = codes_of(own, g)
                at = (0 if own else up_seats) + (g - half_groups) * LANES
                up_mask[pl.ds(at, LANES)] = gather_mask(col)
                up_placed[:, pl.ds(at, LANES)] = (
                    (row // 8 == iota((lists_here, LANES), 0)).astype(F32).astype(BF16)
                )
                up_weights.append((col[:, :1] % 8).astype(F32))

    for c in range(CHUNKS):
        relay(c)
        if c == 0:
            lower_group(0)
    for g in range(1, half_groups):
        lower_group(g)
    upper_codes()

    def up_part(ref, c):
        return ref[c].reshape(up_seats, chunk).astype(F32)

    sq = [jnp.zeros((up_seats, 1), F32), jnp.zeros((up_seats, 1), F32)]
    for c in range(CHUNKS):
        span = pl.ds(c * chunk, chunk)
        for h in range(2):
            for j in range(max(h * (upper // 2), 1), (h + 1) * (upper // 2)):
                relay_copy(c, j).wait_recv()
            forward_up(c, h).start()
        centre = dot(up_mask[...], cent_hi[:, span]) + dot(up_mask[...], cent_lo[:, span])
        diff = up_part(up_rows, c) - centre[:up_seats]
        sq[0] = sq[0] + jnp.sum(diff * diff, axis=1, keepdims=True)
        for h in range(2):
            forward_up(c, h).wait_recv()
        diff = up_part(sib_up, c) - centre[up_seats:]
        sq[1] = sq[1] + jnp.sum(diff * diff, axis=1, keepdims=True)
    share, share_two = shares_of(jnp.concatenate(up_weights, axis=0), jnp.concatenate(sq, axis=0))
    tot[...] += dot(up_placed[...], share_two)
    for c in range(CHUNKS):
        span = pl.ds(c * chunk, chunk)
        got = jnp.concatenate([up_part(up_rows, c), up_part(sib_up, c)], axis=0)
        sv_hi, sv_lo = split_two(share * got)
        acc[:, span] += dot(up_placed[...], sv_hi) + dot(up_placed[...], sv_lo)

    scale = 1.0 / (1.0 + jnp.sum(tot[...], axis=1, keepdims=True))
    refined = acc[...] * scale
    refined_ref[...] = refined
    hi, lo = split_two(refined)
    cent_hi[...] = hi
    cent_lo[...] = lo
    for g in reversed(range(groups)):
        _, col = codes_of(True, g)
        mask = gather_mask(col)
        centre = dot(mask, cent_hi[...]) + dot(mask, cent_lo[...])
        if g < half_groups:
            got = rows[pl.ds(g * per_group, per_group)].reshape(LANES, feature_dim)
        else:
            span = pl.ds((g - half_groups) * per_group, per_group)
            got = jnp.concatenate(
                [up_rows[c, span].reshape(LANES, chunk) for c in range(CHUNKS)], axis=1
            )
        got = got.astype(F32)
        diff = got - centre
        value = jnp.sum(diff * diff, axis=1, keepdims=True) / feature_dim
        back_send[g] = jnp.transpose(jnp.broadcast_to(value, (LANES, LANES)))[:1]
        if g == 0:
            back[0] = back_send[0]
        for j in range(max(g * per_group, 1), (g + 1) * per_group):
            back_copy(j).start()

    seats_lane = seat_keep[...]
    seats_int = seats_lane.astype(jnp.int32)
    for j in range(1, owners):
        back_copy(j).wait_recv()
    spread = [meta_row(back, g) for g in range(groups)]
    out = jnp.zeros((row_count, LANES), F32)
    for k in range(slot_count):
        seat = seats_int[:, k : k + 1]
        chosen = jnp.zeros((row_count, LANES), F32)
        for g in range(groups):
            chosen = jnp.where(lane + g * LANES == seat, spread[g], chosen)
        out = jnp.where(lane == k, jnp.sum(chosen, axis=1, keepdims=True), out)
    dist_ref[...] = jnp.transpose(out)[:slot_count]

    for j in range(1, owners):
        meta_copy(j).wait_send()
        back_copy(j).wait_send()
    for j in range(1, upper):
        row_copy(j).wait_send()
    for c in range(CHUNKS):
        raw_copy(c).wait_send()
        for h in range(2):
            forward_up(c, h).wait_send()
        for j in range(1, upper):
            relay_copy(c, j).wait_send()
    seat_copy.wait_send()
    for g in range(groups):
        forward_meta(g).wait_send()
    for g in range(half_groups):
        forward_copy(g).wait_send()


def shards(vectors, list_ids, spill_weight, list_pos, old_centroids):
    owners = lax.axis_size("grp")
    row_count, slot_count = list_ids.shape
    feature_dim = vectors.shape[1]
    lists_here = old_centroids.shape[0]
    cap = row_count * slot_count // (2 * owners)
    if cap % 16 or LANES % cap or row_count != LANES or owners & (owners - 1) or lists_here % LANES or owners * cap % (2 * LANES):
        return shards_general(vectors, list_ids, spill_weight, list_pos, old_centroids)
    if feature_dim % (CHUNKS * LANES):
        return shards_general(vectors, list_ids, spill_weight, list_pos, old_centroids)
    groups = owners * cap // LANES
    vmem = pl.BlockSpec(memory_space=pltpu.VMEM)
    dma = pltpu.SemaphoreType.DMA
    refined, dist = pl.pallas_call(
        functools.partial(fused_kernel, owners, cap),
        out_shape=(
            pltpu.VMEM((lists_here, feature_dim), F32),
            pltpu.VMEM((slot_count, row_count), F32),
        ),
        in_specs=[vmem, vmem, vmem, vmem, pl.BlockSpec(memory_space=pl.ANY)],
        out_specs=(vmem, vmem),
        scratch_shapes=[
            pltpu.VMEM((lists_here, feature_dim), F32),
            pltpu.VMEM((lists_here, feature_dim), BF16),
            pltpu.VMEM((lists_here, feature_dim), BF16),
            pltpu.VMEM((owners // 2, cap, feature_dim), BF16),
            pltpu.VMEM((groups, 1, LANES), F32),
            pltpu.VMEM((owners // 2, cap, feature_dim), BF16),
            pltpu.VMEM((owners, 1, LANES), F32),
            pltpu.VMEM((owners // 2, cap, feature_dim), BF16),
            pltpu.VMEM((owners, 1, LANES), F32),
            pltpu.VMEM((lists_here, feature_dim), F32),
            pltpu.VMEM((lists_here, LANES), F32),
            pltpu.VMEM((groups, 1, LANES), F32),
            pltpu.VMEM((owners, 1, LANES), F32),
            pltpu.VMEM((row_count, LANES), F32),
            pltpu.VMEM((CHUNKS, owners // 2, cap, feature_dim // CHUNKS), BF16),
            pltpu.VMEM((CHUNKS, owners // 2, cap, feature_dim // CHUNKS), BF16),
            pltpu.VMEM((CHUNKS, owners // 2, cap, feature_dim // CHUNKS), BF16),
            pltpu.VMEM((CHUNKS, row_count, feature_dim // CHUNKS), BF16),
            pltpu.VMEM((slot_count, row_count), F32),
            pltpu.VMEM((slot_count, row_count), F32),
            pltpu.VMEM((owners * cap, lists_here), BF16),
            pltpu.VMEM((lists_here, owners * cap), BF16),
            dma(()),
            dma((CHUNKS,)), dma((CHUNKS,)), dma(()), dma(()),
            dma((CHUNKS, owners // 2)), dma((CHUNKS, owners // 2)), dma((CHUNKS, 2)), dma((CHUNKS, 2)),
            dma((owners,)), dma((owners,)), dma((owners,)), dma((owners,)),
            dma((groups,)), dma((groups,)), dma((groups,)), dma((groups,)),
            dma((owners,)), dma((owners,)),
        ],
        compiler_params=pltpu.CompilerParams(collective_id=0, has_side_effects=True),
    )(vectors, list_ids.T, spill_weight.T, list_pos.reshape(-1, LANES), old_centroids)
    return refined, dist.T


def solution(mesh):
    return jax.shard_map(
        shards,
        mesh=mesh,
        in_specs=(
            P(("grp", "rep"), None),
            P(("grp", "rep"), None),
            P(("grp", "rep"), None),
            P(),
            P("grp", None),
        ),
        out_specs=(P("grp", None), P(("grp", "rep"), None)),
        check_vma=False,
    )
```

profile of v0, /device:TPU:0, one launch (start us, length us, event | category | flops | bytes accessed | tf_op | source)
XLA Modules:
  0.0 37.2 jit_solution(2497270795722934448)
XLA Ops:
  0.6 34.8 %shard_map.68 = (f32[512,768]{1,0:T(8,128)S(1)}, f32[8,128]{1,0:T(8,128)S(1)}) custom-call(bf16[128,768]{1,0:T(8,128)(2,1)} %vec_ref.1, s32[8,128]{1,0:T(8,128)} %bitcast.6, s32[8,128]{1,0:T(8,128)} %bitcast.7, s32[64,128]{1,0:T(8,128)} %bitcast.5, f32[512,768]{1,0:T(8,128)} %cent_hbm.1), custom_call_target="tpu_custom_call" | custom-call | tf_op jit(solution)/shard_map/pallas_call | solution.py:533
  35.4 1.1 %copy.9 = f32[512,768]{1,0:T(8,128)} copy(f32[512,768]{1,0:T(8,128)S(1)} %get-tuple-element.6) | data formatting | bytes 3145728
  36.6 0.6 %copy.10 = f32[128,8]{0,1:T(8,128)} copy(f32[128,8]{0,1:T(8,128)S(1)} %bitcast.4) | data formatting | bytes 8192
where the time goes:
time: 37.3 us; the launch traced here: 37.2 us
  Pallas kernels  34.8 us (93%)
  local copies, waits for them, and re-layouts  1.74 us (5%)
  between operations  0.64 us (2%)
    pallas_call x1, Pallas kernels, shards(): pl.pallas_call(functools.partial(fused_kernel, owners, cap), out_shape=(p...  34.8 us
    unnamed x2, local copies, waits for them, and re-layouts  1.74 us

commit v1 on v0

--- a/solution.py
+++ b/solution.py
@@ -175,7 +175,7 @@
     vec_ref, ids_ref, weight_ref, pos_ref, cent_hbm,
     refined_ref, dist_ref,
     cent, cent_hi, cent_lo, send_buf, meta_send, rows, metas, sib_rows, sib_metas,
-    acc, tot, back_send, back, seat_keep, send_up, up_rows, sib_up, raw_in, seat_out, seat_in, up_mask, up_placed,
+    acc, tot, back_send, back, send_up, up_rows, sib_up, raw_in, seat_out, seat_in, up_mask, up_placed,
     local_sem, s_raw, r_raw, s_seat, r_seat, s_up, r_up, s_fup, r_fup, s_rows, r_rows, s_meta, r_meta, s_fwd, r_fwd, s_fmeta, r_fmeta, s_back, r_back,
 ):
     me = lax.axis_index("grp")
@@ -212,27 +212,22 @@
 
     table = pos_ref[...]
     table_rows = table.shape[0]
-    table_bytes = jnp.concatenate([table // 256, table % 256], axis=1).astype(F32).astype(BF16)
-    ids = jnp.transpose(ids_ref[...])
+    raw_ids = ids_ref[...]
+    safe_ids = jnp.maximum(raw_ids, 0)
+    found = jnp.zeros((slot_count, row_count), jnp.int32)
+    for r in range(table_rows):
+        line = jnp.broadcast_to(table[r : r + 1], (slot_count, LANES))
+        taken = jnp.take_along_axis(line, safe_ids % LANES, axis=1, mode="promise_in_bounds")
+        found = jnp.where(safe_ids // LANES == r, taken, found)
+    ids = jnp.transpose(raw_ids)
     weights = jnp.transpose(weight_ref[...])
+    places = jnp.transpose(found)
     lane = iota((row_count, LANES), 1)
     id_cols = [ids[:, k : k + 1] for k in range(slot_count)]
-    hi_one = jnp.concatenate(
-        [
-            (iota((row_count, table_rows), 1) == jnp.maximum(c, 0) // LANES).astype(F32).astype(BF16)
-            for c in id_cols
-        ],
-        axis=0,
-    )
-    looked = dot(hi_one, table_bytes)
-    place_values = looked[:, :LANES] * 256.0 + looked[:, LANES:]
     live_cols, owner_cols, code_cols = [], [], []
     for k in range(slot_count):
         c = id_cols[k]
-        part = place_values[k * row_count : (k + 1) * row_count]
-        place = jnp.sum(
-            jnp.where(lane == jnp.maximum(c, 0) % LANES, part, 0.0), axis=1, keepdims=True
-        ).astype(jnp.int32)
+        place = places[:, k : k + 1]
         owner = place // lists_here
         live_cols.append(c >= 0)
         owner_cols.append(jnp.where(c >= 0, owner ^ me, -1))
@@ -252,7 +247,6 @@
         seat = jnp.where(live_cols[k], owner_cols[k].astype(F32) * cap + rank, -1.0)
         seat_cols.append(seat)
         seats_lane = jnp.where(lane == k, seat, seats_lane)
-    seat_keep[...] = seats_lane
     seat_rows = jnp.transpose(seats_lane)
     seat_out[...] = seat_rows[:slot_count]
 
@@ -485,19 +479,17 @@
         for j in range(max(g * per_group, 1), (g + 1) * per_group):
             back_copy(j).start()
 
-    seats_lane = seat_keep[...]
-    seats_int = seats_lane.astype(jnp.int32)
+    seats_int = seat_out[...].astype(jnp.int32)
     for j in range(1, owners):
         back_copy(j).wait_recv()
     spread = [meta_row(back, g) for g in range(groups)]
-    out = jnp.zeros((row_count, LANES), F32)
-    for k in range(slot_count):
-        seat = seats_int[:, k : k + 1]
-        chosen = jnp.zeros((row_count, LANES), F32)
-        for g in range(groups):
-            chosen = jnp.where(lane + g * LANES == seat, spread[g], chosen)
-        out = jnp.where(lane == k, jnp.sum(chosen, axis=1, keepdims=True), out)
-    dist_ref[...] = jnp.transpose(out)[:slot_count]
+    out = jnp.zeros((slot_count, row_count), F32)
+    for g in range(groups):
+        line = jnp.broadcast_to(spread[g], (slot_count, LANES))
+        at = jnp.maximum(seats_int, 0) % LANES
+        taken = jnp.take_along_axis(line, at, axis=1, mode="promise_in_bounds")
+        out = jnp.where((seats_int >= 0) & (seats_int // LANES == g), taken, out)
+    dist_ref[...] = out
 
     for j in range(1, owners):
         meta_copy(j).wait_send()
@@ -552,7 +544,6 @@
             pltpu.VMEM((lists_here, LANES), F32),
             pltpu.VMEM((groups, 1, LANES), F32),
             pltpu.VMEM((owners, 1, LANES), F32),
-            pltpu.VMEM((row_count, LANES), F32),
             pltpu.VMEM((CHUNKS, owners // 2, cap, feature_dim // CHUNKS), BF16),
             pltpu.VMEM((CHUNKS, owners // 2, cap, feature_dim // CHUNKS), BF16),
             pltpu.VMEM((CHUNKS, owners // 2, cap, feature_dim // CHUNKS), BF16),

time: 37.3 us -> 36.2 us (0.971)
  Pallas kernels: 34.8 us -> 33.7 us
    pallas_call x1, Pallas kernels: 34.8 us -> 33.7 us  [shards(): pl.pallas_call(functools.partial(fused_kernel, owners, cap), out_shape=(p...]
where the time goes in v1:
time: 36.2 us; the launch traced here: 36.1 us
  Pallas kernels  33.7 us (93%)
  local copies, waits for them, and re-layouts  1.74 us (5%)
  between operations  0.64 us (2%)
    pallas_call x1, Pallas kernels, shards(): pl.pallas_call(functools.partial(fused_kernel, owners, cap), out_shape=(p...  33.7 us
    unnamed x2, local copies, waits for them, and re-layouts  1.74 us

profile of v1, /device:TPU:0, one launch (start us, length us, event | category | flops | bytes accessed | tf_op | source)
XLA Modules:
  0.0 36.1 jit_solution(17307796811379336643)
XLA Ops:
  0.6 33.7 %shard_map.68 = (f32[512,768]{1,0:T(8,128)S(1)}, f32[8,128]{1,0:T(8,128)S(1)}) custom-call(bf16[128,768]{1,0:T(8,128)(2,1)} %vec_ref.1, s32[8,128]{1,0:T(8,128)} %bitcast.6, s32[8,128]{1,0:T(8,128)} %bitcast.7, s32[64,128]{1,0:T(8,128)} %bitcast.5, f32[512,768]{1,0:T(8,128)} %cent_hbm.1), custom_call_target="tpu_custom_call" | custom-call | tf_op jit(solution)/shard_map/pallas_call | solution.py:525
  34.3 1.1 %copy.9 = f32[512,768]{1,0:T(8,128)} copy(f32[512,768]{1,0:T(8,128)S(1)} %get-tuple-element.6) | data formatting | bytes 3145728
  35.5 0.6 %copy.10 = f32[128,8]{0,1:T(8,128)} copy(f32[128,8]{0,1:T(8,128)S(1)} %bitcast.4) | data formatting | bytes 8192

commit v2 on v1

v2 whole, which is shorter than its diff:
```python
import functools
import math

import jax
import jax.numpy as jnp
from jax import lax
from jax.experimental import pallas as pl
from jax.experimental.pallas import tpu as pltpu
from jax.sharding import PartitionSpec as P

D = 768


def decode_meta(meta_rows):
    values = meta_rows.astype(jnp.int32)
    tag_value = values[:, 0] * 128 + values[:, 1]
    return (tag_value > 0, jnp.maximum(tag_value - 1, 0), values[:, 2].astype(jnp.float32))


def pick_block(table, index_block):
    table_iota = jnp.arange(table.shape[0], dtype=jnp.int32)
    if table.dtype == jnp.float32:
        selector = (index_block[:, None] == table_iota[None, :]).astype(jnp.float32)
        return jnp.dot(
            selector, table, precision=lax.Precision.HIGHEST, preferred_element_type=jnp.float32
        )
    selector = (index_block[:, None] == table_iota[None, :]).astype(table.dtype)
    return jnp.dot(selector, table, preferred_element_type=jnp.float32).astype(table.dtype)


def pick_rows(table, indices):
    total_rows = indices.shape[0]
    block_rows = math.gcd(512, total_rows)
    block_count = total_rows // block_rows
    picked = lax.map(
        lambda index_block: pick_block(table, index_block), indices.reshape(block_count, block_rows)
    )
    return picked.reshape(total_rows, table.shape[1])


def owner_sums(rows_all, slot_all, weight_all, old_centroids, lists_here):
    total_rows, feature_dim = rows_all.shape
    block_rows = math.gcd(512, total_rows)
    block_count = total_rows // block_rows
    row_blocks = rows_all.reshape(block_count, block_rows, feature_dim)
    slot_blocks = slot_all.reshape(block_count, block_rows)
    weight_blocks = weight_all.reshape(block_count, block_rows)
    list_iota = jnp.arange(lists_here, dtype=jnp.int32)

    def accumulate(running, piece_item):
        weighted_sums, totals = running
        rows_in, slot_in, weight_in = piece_item
        row_values = rows_in.astype(jnp.float32)
        centre_rows = pick_block(old_centroids, slot_in)
        sq_norms = jnp.sum((row_values - centre_rows) ** 2, axis=-1)
        shares = weight_in / (1.0 + sq_norms / D)
        placed = (slot_in[None, :] == list_iota[:, None]).astype(jnp.float32) * shares[None, :]
        weighted_sums = weighted_sums + jnp.dot(
            placed, row_values, precision=lax.Precision.HIGHEST, preferred_element_type=jnp.float32
        )
        totals = totals + jnp.sum(placed, axis=1)
        return ((weighted_sums, totals), jnp.float32(0.0))

    start_state = (
        jnp.zeros((lists_here, feature_dim), jnp.float32),
        jnp.zeros((lists_here,), jnp.float32),
    )
    final_state, unused = lax.scan(
        accumulate, start_state, (row_blocks, slot_blocks, weight_blocks)
    )
    return final_state


def shards_general(vectors, list_ids, spill_weight, list_pos, old_centroids):
    owners = lax.axis_size("grp")
    row_count, slot_count = list_ids.shape
    feature_dim = vectors.shape[1]
    lists_here = old_centroids.shape[0]
    cap_slots = row_count * slot_count // (2 * owners)
    seat_total = owners * cap_slots
    pair_count = row_count * slot_count
    is_live = list_ids >= 0
    places = jnp.where(is_live, list_pos[jnp.maximum(list_ids, 0)], 0)
    target = jnp.where(is_live, places // lists_here, owners).reshape(-1)
    sorted_order = jnp.argsort(target, stable=True)
    ranked = target[sorted_order]
    counts = jnp.sum(
        (target[:, None] == jnp.arange(owners, dtype=jnp.int32)[None, :]).astype(jnp.int32), axis=0
    )
    starts = jnp.concatenate([jnp.cumsum(counts) - counts, jnp.zeros((1,), jnp.int32)])
    within = jnp.arange(pair_count, dtype=jnp.int32) - starts[ranked]
    seat_sorted = jnp.where(ranked < owners, ranked * cap_slots + within, seat_total)
    seat_index = jnp.zeros((pair_count,), jnp.int32).at[sorted_order].set(seat_sorted)
    pair_of_seat = (
        jnp.full((seat_total,), -1, jnp.int32)
        .at[seat_index]
        .set(jnp.arange(pair_count, dtype=jnp.int32), mode="drop")
    )
    filled = pair_of_seat >= 0
    pair_safe = jnp.maximum(pair_of_seat, 0)
    source_row = jnp.where(filled, pair_safe // slot_count, -1)
    send_rows = pick_rows(vectors, source_row)
    local_flat = (places % lists_here).reshape(-1)
    weight_flat = spill_weight.reshape(-1)
    tag_out = jnp.where(filled, local_flat[pair_safe] + 1, 0)
    weight_out = jnp.where(filled, weight_flat[pair_safe], 0)
    send_meta = jnp.stack([tag_out // 128, tag_out % 128, weight_out], axis=-1).astype(jnp.bfloat16)
    got_rows, got_meta = (
        lax.all_to_all(
            send_rows.reshape(owners, cap_slots, feature_dim),
            "grp",
            split_axis=0,
            concat_axis=0,
            tiled=True,
        ),
        lax.all_to_all(
            send_meta.reshape(owners, cap_slots, 3), "grp", split_axis=0, concat_axis=0, tiled=True
        ),
    )
    got_rows = got_rows.reshape(seat_total, feature_dim)
    got_meta = got_meta.reshape(seat_total, 3)
    seat_live, seat_row, seat_weight = decode_meta(got_meta)
    weighted_sums, totals = owner_sums(got_rows, seat_row, seat_weight, old_centroids, lists_here)
    weighted_sums, totals = lax.psum((weighted_sums, totals), "rep")
    refined = (old_centroids + weighted_sums) / (1.0 + totals[:, None])
    block_rows = math.gcd(512, seat_total)
    block_count = seat_total // block_rows
    row_blocks = got_rows.reshape(block_count, block_rows, feature_dim)
    slot_blocks = seat_row.reshape(block_count, block_rows)

    def distance(piece_item):
        rows_in, slot_in = piece_item
        row_values = rows_in.astype(jnp.float32)
        return jnp.sum((row_values - pick_block(refined, slot_in)) ** 2, axis=-1) / D

    owner_dist = lax.map(distance, (row_blocks, slot_blocks)).reshape(owners, cap_slots)
    seat_dist = lax.all_to_all(owner_dist, "grp", split_axis=0, concat_axis=0, tiled=True).reshape(
        seat_total
    )
    picked = seat_dist[jnp.minimum(seat_index, seat_total - 1)].reshape(row_count, slot_count)
    new_dist = jnp.where(is_live, picked, jnp.float32(0.0))
    return (refined, new_dist)


MESH = pl.DeviceIdType.MESH
LANES = 128
LINE = 4
F32 = jnp.float32
BF16 = jnp.bfloat16


def xor_index(a, b_const, bits):
    out = 0
    for i in range(bits):
        bit = (a // (1 << i)) % 2
        out = out + ((1 - bit) if (b_const >> i) & 1 else bit) * (1 << i)
    return out


def split_two(x):
    hi = x.astype(BF16)
    return hi, (x - hi.astype(F32)).astype(BF16)


def dot(a, b):
    return jnp.dot(a, b, preferred_element_type=F32)


def iota(shape, dim):
    return lax.broadcasted_iota(jnp.int32, shape, dim)


def take_lanes(line, at):
    wide = jnp.broadcast_to(line, at.shape)
    return jnp.take_along_axis(wide, at, axis=1, mode="promise_in_bounds")


def line_kernel(
    owners, cap,
    vec_hbm, ids_hbm, weight_hbm, pos_hbm, cent_hbm,
    refined_ref, dist_ref,
    ints, vec_other, cent, cent_cat, raw_in, meta_in, seat_keep, send_buf, rows, codes,
    masks, placed, sq_own, sq_sib, acc, tot, back_send, back,
    l_sem, s_own, s_meta, r_raw, r_meta, s_row, r_row, s_code, r_code, s_sq, r_sq, s_back, r_back, s_ref, r_ref,
):
    me = lax.axis_index("grp")
    rep = lax.axis_index("rep")
    slot_count, row_count = seat_keep.shape
    lists_here, half = cent.shape
    table_rows = pos_hbm.shape[0]
    plane = owners // LINE
    pbits = plane.bit_length() - 1
    z = me // plane
    p = me % plane
    mid = ((z + 1) // 2) % 2
    near = z + 1 - 2 * (z % 2)
    inner = LINE - 1 - z
    cross = (z + 2) % LINE
    z_of = [z, near, mid * inner + (1 - mid) * cross, mid * cross + (1 - mid) * inner]
    xz_of = [0, 1, 2 + mid, 3 - mid]
    rep_of = [rep, 1 - rep]
    mine = pl.ds(pl.multiple_of(rep * half, LANES), half)
    theirs = pl.ds(pl.multiple_of((1 - rep) * half, LANES), half)

    def at(place, xp):
        return place * plane + xor_index(p, xp, pbits)

    barrier = pltpu.get_barrier_semaphore()

    def greet(place, xp, r):
        pl.semaphore_signal(barrier, inc=1, device_id={"grp": at(place, xp), "rep": r}, device_id_type=MESH)

    greet(near, 0, 0)
    greet(near, 0, 1)

    @pl.when(mid == 1)
    def _():
        greet(inner, 0, 0)
        greet(inner, 0, 1)

    for j in range(1, plane):
        greet(z, j, rep)
    greet(z, 0, 1 - rep)

    local = [
        pltpu.make_async_copy(vec_hbm.at[:, mine], raw_in.at[0, 0], l_sem.at[0]),
        pltpu.make_async_copy(vec_hbm.at[:, theirs], vec_other, l_sem.at[1]),
        pltpu.make_async_copy(ids_hbm, ints.at[pl.ds(0, slot_count)], l_sem.at[2]),
        pltpu.make_async_copy(weight_hbm, ints.at[pl.ds(slot_count, slot_count)], l_sem.at[2]),
        pltpu.make_async_copy(pos_hbm, ints.at[pl.ds(2 * slot_count, table_rows)], l_sem.at[2]),
        pltpu.make_async_copy(cent_hbm.at[:, mine], cent, l_sem.at[3]),
    ]
    for copy in local:
        copy.start()

    def remote(src, dst, send, recv, place, xp, r):
        return pltpu.make_async_remote_copy(
            src_ref=src, dst_ref=dst, send_sem=send, recv_sem=recv,
            device_id={"grp": at(place, xp), "rep": r}, device_id_type=MESH,
        )

    own_place = [z, near, inner]
    others = pl.ds(1, plane - 1)

    def own_raw(s, f):
        src = raw_in.at[0, 0] if f == 0 else vec_other
        return remote(src, raw_in.at[s, f], s_own.at[s // 2], r_raw.at[s, f], own_place[s], 0, rep_of[f])

    def own_meta(s, f):
        return remote(
            meta_in.at[0, 0], meta_in.at[s, f], s_meta.at[s // 2], r_meta.at[s, f], own_place[s], 0, rep_of[f]
        )

    forward_to = {1: (3, inner), 2: (2, near), 3: (3, near)}

    def forward(s, f):
        to, place = forward_to[s]
        return (
            remote(meta_in.at[s, f], meta_in.at[to, f], s_meta.at[1], r_meta.at[to, f], place, 0, rep),
            remote(raw_in.at[s, f], raw_in.at[to, f], s_own.at[1], r_raw.at[to, f], place, 0, rep),
        )

    def row_copy(s, f, j):
        return remote(send_buf.at[s, f, j], rows.at[s, f, j], s_row, r_row.at[s], z, j, rep)

    def code_copy(s, f, j):
        src = meta_in.at[s, f, slot_count + xz_of[s]]
        return remote(src, codes.at[s, f, j], s_code, r_code.at[s], z, j, rep)

    def sq_copy(s):
        return remote(sq_own.at[s], sq_sib.at[s], s_sq, r_sq.at[s], z, 0, 1 - rep)

    def back_copy(s, f, j):
        to = back.at[(xz_of[s] * plane + j) * 2 + f]
        return remote(back_send.at[s, f], to, s_back, r_back, z_of[s], j, rep_of[f])

    def arrived(ref, sem):
        pltpu.make_async_copy(ref, ref, sem).wait()

    ref_copy = remote(refined_ref.at[:, mine], refined_ref.at[:, mine], s_ref, r_ref, z, 0, 1 - rep)
    ref_wait = remote(refined_ref.at[:, theirs], refined_ref.at[:, theirs], s_ref, r_ref, z, 0, 1 - rep)

    pl.semaphore_wait(barrier, plane + 2 + 2 * mid)
    local[0].wait()
    own_raw(1, 0).start()

    @pl.when(mid == 1)
    def _():
        own_raw(2, 0).start()

    local[1].wait()
    own_raw(0, 1).start()

    pltpu.make_async_copy(ints, ints, l_sem.at[2]).wait()
    raw_ids = ints[pl.ds(0, slot_count)]
    weights = ints[pl.ds(slot_count, slot_count)]
    table = ints[pl.ds(2 * slot_count, table_rows)]
    live = raw_ids >= 0
    safe_ids = jnp.maximum(raw_ids, 0)
    place = jnp.zeros((slot_count, row_count), jnp.int32)
    for r in range(table_rows):
        taken = take_lanes(table[r : r + 1], safe_ids % LANES)
        place = jnp.where(safe_ids // LANES == r, taken, place)
    owner = place // lists_here
    to_z, to_p = owner // plane, owner % plane

    def xor_two(a, b, bits):
        out = 0
        for i in range(bits):
            out = out + ((a // (1 << i) + b // (1 << i)) % 2) * (1 << i)
        return out

    turned = xor_two(to_z, z, 2) * plane + xor_two(to_p, p, pbits)
    turned = jnp.where(live, turned, -1)
    code = ((place % lists_here) * 8 + weights).astype(F32)
    square = (LANES, LANES)
    lane = iota(square, 1)
    sub = iota(square, 0)
    member = jnp.concatenate([(turned == o).astype(F32) for o in range(owners)], axis=0).astype(BF16)
    earlier = (sub < lane).astype(F32).astype(BF16)
    same_owner = sub // slot_count == lane // slot_count
    prior = (same_owner & (lane < sub)).astype(F32).astype(BF16)
    before = dot(prior, member).astype(BF16)
    rank_all = dot(member, earlier) + dot(before, jnp.ones(square, BF16))
    rank = jnp.zeros((slot_count, row_count), F32)
    for o in range(owners):
        rank = jnp.where(turned == o, rank_all[o * slot_count : (o + 1) * slot_count], rank)
    seat = jnp.where(live, turned.astype(F32) * cap + rank, -1.0)
    seat_keep[...] = seat
    for k in range(slot_count):
        meta_in[0, 0, k] = seat[k : k + 1]
    eye = sub == lane

    def to_row(col):
        return jnp.sum(jnp.where(eye, col, 0.0), axis=0, keepdims=True)

    def to_col(row):
        return jnp.sum(jnp.where(eye, row, 0.0), axis=1, keepdims=True)

    for g in range(LINE):
        q = (sub + g * LANES).astype(F32)
        found = jnp.zeros(square, F32)
        for k in range(slot_count):
            found = found + jnp.where(seat[k : k + 1] == q, code[k : k + 1], 0.0)
        meta_in[0, 0, slot_count + g] = to_row(jnp.sum(found, axis=1, keepdims=True))

    for f in range(2):
        own_meta(1, f).start()
    own_raw(1, 1).start()

    @pl.when(mid == 1)
    def _():
        for f in range(2):
            own_meta(2, f).start()
        own_raw(2, 1).start()

    own_meta(0, 1).start()

    def pick(s, f):
        if (s, f) != (0, 0):
            arrived(meta_in.at[s, f], r_meta.at[s, f])
        for j in range(1, plane):
            code_copy(s, f, j).start()
        if (s, f) != (0, 0):
            arrived(raw_in.at[s, f], r_raw.at[s, f])
        if s:

            @pl.when(mid == 1)
            def _():
                for copy in forward(s, f):
                    copy.start()

        q = (sub + xz_of[s] * LANES).astype(F32)
        chosen = jnp.zeros(square, F32)
        for k in range(slot_count):
            chosen = chosen + (meta_in[s, f, k] == q).astype(F32)
        picked = dot(chosen.astype(BF16), raw_in[s, f]).astype(BF16).reshape(plane, cap, half)
        send_buf[s, f] = picked
        for j in reversed(range(1, plane)):
            row_copy(s, f, j).start()
        rows[s, f, 0] = picked[0]

    lane_row = iota((1, LANES), 1)

    def code_row(s, f):
        out = meta_in[s, f, slot_count + xz_of[s]]
        for j in range(1, plane):
            out = jnp.where(lane_row // cap == j, codes[s, f, j], out)
        return out

    def halves(x):
        return x[:, :half] + x[:, half : 2 * half]

    def lane_parts(x):
        out = x[:, :LANES]
        for i in range(1, half // LANES):
            out = out + x[:, i * LANES : (i + 1) * LANES]
        return out

    def got_rows(s):
        return rows[s].reshape(2 * LANES, half).astype(F32)

    def near_part(s):
        arrived(codes.at[s, :, others], r_code.at[s])
        for f in range(2):
            row = code_row(s, f)
            wide = to_col(row).astype(jnp.int32) // 8
            masks[s, pl.ds(f * LANES, LANES)] = (
                (wide == iota((LANES, lists_here), 1)).astype(F32).astype(BF16)
            )
            placed[s, :, pl.ds(f * LANES, LANES)] = (
                (row.astype(jnp.int32) // 8 == iota((lists_here, LANES), 0)).astype(F32).astype(BF16)
            )
        centre = halves(dot(masks[s], cent_cat[...]))
        arrived(rows.at[s, :, others], r_row.at[s])
        diff = got_rows(s) - centre
        sq_own[s] = lane_parts(diff * diff)
        sq_copy(s).start()

    def far_part(s):
        weight = jnp.concatenate(
            [to_col((code_row(s, f).astype(jnp.int32) % 8).astype(F32)) for f in range(2)], axis=0
        )
        got = got_rows(s)
        sq_copy(s).wait_recv()
        swapped = jnp.concatenate([sq_sib[s, LANES:], sq_sib[s, :LANES]], axis=0)
        sq = jnp.sum(sq_own[s] + swapped, axis=1, keepdims=True)
        share = jnp.broadcast_to(weight / (1.0 + sq / (2 * half)), (2 * LANES, LANES))
        share_hi, share_lo = split_two(share)
        sv_hi, sv_lo = split_two(jnp.concatenate([share] * (half // LANES), axis=1) * got)
        added = dot(placed[s], jnp.concatenate([sv_hi, sv_lo, share_hi, share_lo], axis=1))
        sums = halves(added)
        counts = added[:, 2 * half : 2 * half + LANES] + added[:, 2 * half + LANES :]
        acc[...] = (cent[...] if s == 0 else acc[...]) + sums
        tot[...] = counts if s == 0 else tot[...] + counts

    pick(0, 0)
    local[5].wait()
    hi, lo = split_two(cent[...])
    cent_cat[:, pl.ds(0, half)] = hi
    cent_cat[:, pl.ds(half, half)] = lo
    pick(0, 1)

    def follow(steps):
        for step, args in steps:
            step(*args)

    @pl.when(mid == 1)
    def _():
        follow([
            (pick, (2, 0)), (pick, (1, 0)), (pick, (2, 1)), (pick, (1, 1)), (near_part, (0,)), (pick, (3, 0)), (pick, (3, 1)),
            (far_part, (0,)), (near_part, (1,)), (near_part, (2,)), (far_part, (1,)), (near_part, (3,)), (far_part, (2,)),
            (far_part, (3,)),
        ])

    @pl.when(mid == 0)
    def _():
        follow([
            (pick, (1, 0)), (pick, (1, 1)), (near_part, (0,)), (pick, (2, 0)), (near_part, (1,)), (far_part, (0,)), (pick, (2, 1)),
            (far_part, (1,)), (pick, (3, 0)), (near_part, (2,)), (pick, (3, 1)), (near_part, (3,)), (far_part, (2,)),
            (far_part, (3,)),
        ])

    scale = 1.0 / (1.0 + tot[...])
    refined = acc[...] * jnp.concatenate([scale] * (half // LANES), axis=1)
    refined_ref[:, mine] = refined
    hi, lo = split_two(refined)
    cent_cat[:, pl.ds(0, half)] = hi
    cent_cat[:, pl.ds(half, half)] = lo

    for s in reversed(range(LINE)):
        diff = got_rows(s) - halves(dot(masks[s], cent_cat[...]))
        value = jnp.sum(lane_parts(diff * diff), axis=1, keepdims=True) / (2 * half)
        for f in range(2):
            row = to_row(value[f * LANES : (f + 1) * LANES])
            back_send[s, f] = row
            for j in range(plane):
                if (s, f, j) != (0, 0, 0):
                    back_copy(s, f, j).start()
            if (s, f) == (0, 0):
                back[0] = row
        if s == 2:
            ref_copy.start()

    seats = seat_keep[...].astype(jnp.int32)
    lanes_at = jnp.maximum(seats, 0) % LANES
    out = jnp.zeros((slot_count, row_count), F32)
    arrived(back.at[pl.ds(1, 2 * owners - 1)], r_back)
    for x in range(LINE):
        line = jnp.zeros((1, LANES), F32)
        for j in range(plane):
            first = (x * plane + j) * 2
            line = jnp.where(lane_row // cap == j, back[first] + back[first + 1], line)
        taken = take_lanes(line, lanes_at)
        out = jnp.where((seats >= 0) & (seats // LANES == x), taken, out)
    dist_ref[...] = out

    ref_wait.wait_recv()
    ref_copy.wait_send()
    arrived(raw_in.at[pl.ds(0, 3), 0], s_own.at[0])
    arrived(meta_in.at[pl.ds(0, 3), 0], s_meta.at[0])

    @pl.when(mid == 1)
    def _():
        arrived(raw_in, s_own.at[1])
        arrived(meta_in, s_meta.at[1])

    arrived(sq_own, s_sq)
    arrived(rows.at[:, :, others], s_row)
    arrived(codes.at[:, :, others], s_code)
    arrived(back.at[pl.ds(1, 2 * owners - 1)], s_back)


def shards(vectors, list_ids, spill_weight, list_pos, old_centroids):
    owners = lax.axis_size("grp")
    row_count, slot_count = list_ids.shape
    feature_dim = vectors.shape[1]
    lists_here = old_centroids.shape[0]
    cap = row_count * slot_count // (2 * owners)
    plane = owners // LINE
    fits = (
        row_count == LANES and slot_count == 8 and owners * cap == LINE * LANES and plane & (plane - 1) == 0
        and owners * slot_count == LANES and cap % 16 == 0 and lax.axis_size("rep") == 2
        and lists_here % LANES == 0 and feature_dim % (2 * LANES) == 0 and list_pos.shape[0] % LANES == 0
    )
    if not fits:
        return shards_general(vectors, list_ids, spill_weight, list_pos, old_centroids)
    half = feature_dim // 2
    table_rows = list_pos.shape[0] // LANES
    meta_rows = slot_count + LINE
    vmem = pl.BlockSpec(memory_space=pltpu.VMEM)
    hbm = pl.BlockSpec(memory_space=pl.ANY)
    dma = pltpu.SemaphoreType.DMA
    refined, dist = pl.pallas_call(
        functools.partial(line_kernel, owners, cap),
        out_shape=(
            pltpu.VMEM((lists_here, feature_dim), F32),
            pltpu.VMEM((slot_count, row_count), F32),
        ),
        in_specs=[hbm] * 5,
        out_specs=(vmem, vmem),
        scratch_shapes=[
            pltpu.VMEM((2 * slot_count + table_rows, LANES), jnp.int32),
            pltpu.VMEM((row_count, half), BF16),
            pltpu.VMEM((lists_here, half), F32),
            pltpu.VMEM((lists_here, feature_dim), BF16),
            pltpu.VMEM((LINE, 2, row_count, half), BF16),
            pltpu.VMEM((LINE, 2, meta_rows, 1, LANES), F32),
            pltpu.VMEM((slot_count, row_count), F32),
            pltpu.VMEM((LINE, 2, plane, cap, half), BF16),
            pltpu.VMEM((LINE, 2, plane, cap, half), BF16),
            pltpu.VMEM((LINE, 2, plane, 1, LANES), F32),
            pltpu.VMEM((LINE, 2 * LANES, lists_here), BF16),
            pltpu.VMEM((LINE, lists_here, 2 * LANES), BF16),
            pltpu.VMEM((LINE, 2 * LANES, LANES), F32),
            pltpu.VMEM((LINE, 2 * LANES, LANES), F32),
            pltpu.VMEM((lists_here, half), F32),
            pltpu.VMEM((lists_here, LANES), F32),
            pltpu.VMEM((LINE, 2, 1, LANES), F32),
            pltpu.VMEM((2 * owners, 1, LANES), F32),
            dma((4,)),
            dma((2,)), dma((2,)), dma((LINE, 2)), dma((LINE, 2)),
            dma(()), dma((LINE,)), dma(()), dma((LINE,)), dma(()), dma((LINE,)),
            dma(()), dma(()), dma(()), dma(()),
        ],
        compiler_params=pltpu.CompilerParams(collective_id=0, has_side_effects=True),
    )(vectors, list_ids.T, spill_weight.T, list_pos.reshape(-1, LANES), old_centroids)
    return refined, dist.T


def solution(mesh):
    return jax.shard_map(
        shards,
        mesh=mesh,
        in_specs=(
            P(("grp", "rep"), None),
            P(("grp", "rep"), None),
            P(("grp", "rep"), None),
            P(),
            P("grp", None),
        ),
        out_specs=(P("grp", None), P(("grp", "rep"), None)),
        check_vma=False,
    )
```

time: 36.2 us -> 33.8 us (0.934)
  Pallas kernels: 33.7 us -> 31.3 us
    pallas_call x1, Pallas kernels: 33.7 us -> 31.3 us  [shards(): pl.pallas_call(functools.partial(line_kernel, owners, cap), out_shape=(pl...]
where the time goes in v2:
time: 33.8 us; the launch traced here: 33.7 us
  Pallas kernels  31.3 us (93%)
  local copies, waits for them, and re-layouts  1.74 us (5%)
  between operations  0.64 us (2%)
    pallas_call x1, Pallas kernels, shards(): pl.pallas_call(functools.partial(line_kernel, owners, cap), out_shape=(pl...  31.3 us
    unnamed x2, local copies, waits for them, and re-layouts  1.74 us

profile of v2, /device:TPU:0, one launch (start us, length us, event | category | flops | bytes accessed | tf_op | source)
XLA Modules:
  0.0 33.7 jit_solution(10702170430833505374)
XLA Ops:
  0.6 31.3 %shard_map.68 = (f32[512,768]{1,0:T(8,128)S(1)}, f32[8,128]{1,0:T(8,128)S(1)}) custom-call(bf16[128,768]{1,0:T(8,128)(2,1)} %vec_hbm.1, s32[8,128]{1,0:T(8,128)} %bitcast.6, s32[8,128]{1,0:T(8,128)} %bitcast.7, s32[64,128]{1,0:T(8,128)} %bitcast.5, f32[512,768]{1,0:T(8,128)} %cent_hbm.1), custom_call_target="tpu_custom_call" | custom-call | tf_op jit(solution)/shard_map/pallas_call | solution.py:534
  31.9 1.1 %copy.9 = f32[512,768]{1,0:T(8,128)} copy(f32[512,768]{1,0:T(8,128)S(1)} %get-tuple-element.6) | data formatting | bytes 3145728
  33.1 0.6 %copy.10 = f32[128,8]{0,1:T(8,128)} copy(f32[128,8]{0,1:T(8,128)S(1)} %bitcast.4) | data formatting | bytes 8192

commit v3 on v2

--- a/solution.py
+++ b/solution.py
@@ -179,9 +179,9 @@
     owners, cap,
     vec_hbm, ids_hbm, weight_hbm, pos_hbm, cent_hbm,
     refined_ref, dist_ref,
-    ints, vec_other, cent, cent_cat, raw_in, meta_in, seat_keep, send_buf, rows, codes,
+    ints, vec_other, cent, cent_cat, raw_in, meta_in, seat_keep, send_buf, send_near, rows, codes,
     masks, placed, sq_own, sq_sib, acc, tot, back_send, back,
-    l_sem, s_own, s_meta, r_raw, r_meta, s_row, r_row, s_code, r_code, s_sq, r_sq, s_back, r_back, s_ref, r_ref,
+    l_sem, s_own, s_meta, r_raw, r_meta, s_row, r_row, s_code, r_code, s_sq, r_sq, s_back, r_back, s_ref, r_ref, s_near, first, second,
 ):
     me = lax.axis_index("grp")
     rep = lax.axis_index("rep")
@@ -218,8 +218,8 @@
         greet(inner, 0, 0)
         greet(inner, 0, 1)
 
-    for j in range(1, plane):
-        greet(z, j, rep)
+    for i in range(pbits):
+        greet(z, 1 << i, rep)
     greet(z, 0, 1 - rep)
 
     local = [
@@ -233,6 +233,10 @@
     for copy in local:
         copy.start()
 
+    def tell(semaphore, steps):
+        for j in steps:
+            pl.semaphore_signal(semaphore, inc=1, device_id={"grp": at(z, j), "rep": rep}, device_id_type=MESH)
+
     def remote(src, dst, send, recv, place, xp, r):
         return pltpu.make_async_remote_copy(
             src_ref=src, dst_ref=dst, send_sem=send, recv_sem=recv,
@@ -251,13 +255,10 @@
             meta_in.at[0, 0], meta_in.at[s, f], s_meta.at[s // 2], r_meta.at[s, f], own_place[s], 0, rep_of[f]
         )
 
-    forward_to = {1: (3, inner), 2: (2, near), 3: (3, near)}
-
-    def forward(s, f):
-        to, place = forward_to[s]
+    def forward(f):
         return (
-            remote(meta_in.at[s, f], meta_in.at[to, f], s_meta.at[1], r_meta.at[to, f], place, 0, rep),
-            remote(raw_in.at[s, f], raw_in.at[to, f], s_own.at[1], r_raw.at[to, f], place, 0, rep),
+            remote(meta_in.at[1, f], meta_in.at[3, f], s_meta.at[1], r_meta.at[3, f], inner, 0, rep),
+            remote(raw_in.at[1, f], raw_in.at[3, f], s_own.at[1], r_raw.at[3, f], inner, 0, rep),
         )
 
     def row_copy(s, f, j):
@@ -267,6 +268,13 @@
         src = meta_in.at[s, f, slot_count + xz_of[s]]
         return remote(src, codes.at[s, f, j], s_code, r_code.at[s], z, j, rep)
 
+    def near_row_copy(s, f, j):
+        return remote(send_near.at[s - 2, f, j], rows.at[s, f, j], s_own.at[1], r_row.at[s], near, j, rep)
+
+    def near_code_copy(s, f, j):
+        src = meta_in.at[s, f, slot_count + s]
+        return remote(src, codes.at[s, f, j], s_near, r_code.at[s], near, j, rep)
+
     def sq_copy(s):
         return remote(sq_own.at[s], sq_sib.at[s], s_sq, r_sq.at[s], z, 0, 1 - rep)
 
@@ -280,17 +288,19 @@
     ref_copy = remote(refined_ref.at[:, mine], refined_ref.at[:, mine], s_ref, r_ref, z, 0, 1 - rep)
     ref_wait = remote(refined_ref.at[:, theirs], refined_ref.at[:, theirs], s_ref, r_ref, z, 0, 1 - rep)
 
-    pl.semaphore_wait(barrier, plane + 2 + 2 * mid)
+    pl.semaphore_wait(barrier, pbits + 3 + 2 * mid)
+    def own_to(f):
+        own_raw(1, f).start()
+
+        @pl.when(mid == 1)
+        def _():
+            own_raw(2, f).start()
+
+    tell(first, [1 << i for i in range(pbits)])
     local[0].wait()
-    own_raw(1, 0).start()
-
-    @pl.when(mid == 1)
-    def _():
-        own_raw(2, 0).start()
-
+    own_to(0)
     local[1].wait()
     own_raw(0, 1).start()
-
     pltpu.make_async_copy(ints, ints, l_sem.at[2]).wait()
     raw_ids = ints[pl.ds(0, slot_count)]
     weights = ints[pl.ds(slot_count, slot_count)]
@@ -346,44 +356,59 @@
 
     for f in range(2):
         own_meta(1, f).start()
-    own_raw(1, 1).start()
 
     @pl.when(mid == 1)
     def _():
         for f in range(2):
             own_meta(2, f).start()
-        own_raw(2, 1).start()
-
+
+    own_to(1)
     own_meta(0, 1).start()
 
-    def pick(s, f):
-        if (s, f) != (0, 0):
-            arrived(meta_in.at[s, f], r_meta.at[s, f])
-        for j in range(1, plane):
-            code_copy(s, f, j).start()
-        if (s, f) != (0, 0):
-            arrived(raw_in.at[s, f], r_raw.at[s, f])
-        if s:
-
-            @pl.when(mid == 1)
-            def _():
-                for copy in forward(s, f):
-                    copy.start()
-
-        q = (sub + xz_of[s] * LANES).astype(F32)
+    def picked_rows(s, f, xz):
+        q = (sub + xz * LANES).astype(F32)
         chosen = jnp.zeros(square, F32)
         for k in range(slot_count):
             chosen = chosen + (meta_in[s, f, k] == q).astype(F32)
-        picked = dot(chosen.astype(BF16), raw_in[s, f]).astype(BF16).reshape(plane, cap, half)
+        return dot(chosen.astype(BF16), raw_in[s, f]).astype(BF16).reshape(plane, cap, half)
+
+    def pick(s, f):
+        to_near = s >= 2
+        if (s, f) != (0, 0):
+            arrived(meta_in.at[s, f], r_meta.at[s, f])
+        for j in reversed(range(plane)):
+            if to_near:
+                near_code_copy(s, f, j).start()
+            if j and (s, f) != (0, 0):
+                code_copy(s, f, j).start()
+        if (s, f) != (0, 0):
+            arrived(raw_in.at[s, f], r_raw.at[s, f])
+        if to_near:
+            send_near[s - 2, f] = picked_rows(s, f, s)
+            for j in reversed(range(plane)):
+                near_row_copy(s, f, j).start()
+        elif s:
+
+            @pl.when(mid == 1)
+            def _():
+                for copy in forward(f):
+                    copy.start()
+
+        picked = picked_rows(s, f, xz_of[s])
         send_buf[s, f] = picked
+        if (s, f) == (0, 0):
+            pl.semaphore_wait(first, pbits)
+            tell(second, [1])
+            for j in reversed(range(1, plane)):
+                code_copy(s, f, j).start()
         for j in reversed(range(1, plane)):
             row_copy(s, f, j).start()
         rows[s, f, 0] = picked[0]
 
     lane_row = iota((1, LANES), 1)
 
-    def code_row(s, f):
-        out = meta_in[s, f, slot_count + xz_of[s]]
+    def code_row(s, f, picked_here=True):
+        out = meta_in[s, f, slot_count + xz_of[s]] if picked_here else codes[s, f, 0]
         for j in range(1, plane):
             out = jnp.where(lane_row // cap == j, codes[s, f, j], out)
         return out
@@ -400,10 +425,10 @@
     def got_rows(s):
         return rows[s].reshape(2 * LANES, half).astype(F32)
 
-    def near_part(s):
-        arrived(codes.at[s, :, others], r_code.at[s])
+    def near_part(s, picked_here=True):
+        arrived(codes.at[s, :, others] if picked_here else codes.at[s], r_code.at[s])
         for f in range(2):
-            row = code_row(s, f)
+            row = code_row(s, f, picked_here)
             wide = to_col(row).astype(jnp.int32) // 8
             masks[s, pl.ds(f * LANES, LANES)] = (
                 (wide == iota((LANES, lists_here), 1)).astype(F32).astype(BF16)
@@ -412,14 +437,14 @@
                 (row.astype(jnp.int32) // 8 == iota((lists_here, LANES), 0)).astype(F32).astype(BF16)
             )
         centre = halves(dot(masks[s], cent_cat[...]))
-        arrived(rows.at[s, :, others], r_row.at[s])
+        arrived(rows.at[s, :, others] if picked_here else rows.at[s], r_row.at[s])
         diff = got_rows(s) - centre
         sq_own[s] = lane_parts(diff * diff)
         sq_copy(s).start()
 
-    def far_part(s):
+    def far_part(s, picked_here=True):
         weight = jnp.concatenate(
-            [to_col((code_row(s, f).astype(jnp.int32) % 8).astype(F32)) for f in range(2)], axis=0
+            [to_col((code_row(s, f, picked_here).astype(jnp.int32) % 8).astype(F32)) for f in range(2)], axis=0
         )
         got = got_rows(s)
         sq_copy(s).wait_recv()
@@ -447,18 +472,19 @@
 
     @pl.when(mid == 1)
     def _():
+        pl.semaphore_wait(second, 1)
         follow([
-            (pick, (2, 0)), (pick, (1, 0)), (pick, (2, 1)), (pick, (1, 1)), (near_part, (0,)), (pick, (3, 0)), (pick, (3, 1)),
+            (pick, (1, 0)), (pick, (2, 0)), (pick, (1, 1)), (pick, (2, 1)), (near_part, (0,)), (pick, (3, 0)), (pick, (3, 1)),
             (far_part, (0,)), (near_part, (1,)), (near_part, (2,)), (far_part, (1,)), (near_part, (3,)), (far_part, (2,)),
             (far_part, (3,)),
         ])
 
     @pl.when(mid == 0)
     def _():
+        pl.semaphore_wait(second, 1)
         follow([
-            (pick, (1, 0)), (pick, (1, 1)), (near_part, (0,)), (pick, (2, 0)), (near_part, (1,)), (far_part, (0,)), (pick, (2, 1)),
-            (far_part, (1,)), (pick, (3, 0)), (near_part, (2,)), (pick, (3, 1)), (near_part, (3,)), (far_part, (2,)),
-            (far_part, (3,)),
+            (pick, (1, 0)), (pick, (1, 1)), (near_part, (0,)), (near_part, (1,)), (far_part, (0,)), (far_part, (1,)),
+            (near_part, (2, False)), (near_part, (3, False)), (far_part, (2, False)), (far_part, (3, False)),
         ])
 
     scale = 1.0 / (1.0 + tot[...])
@@ -503,12 +529,29 @@
     @pl.when(mid == 1)
     def _():
         arrived(raw_in, s_own.at[1])
-        arrived(meta_in, s_meta.at[1])
+        arrived(meta_in.at[pl.ds(0, 2)], s_meta.at[1])
+        arrived(rows.at[:, :, others], s_row)
+        arrived(codes.at[:, :, others], s_code)
+        arrived(codes.at[pl.ds(2, 2)], s_near)
+
+    @pl.when(mid == 0)
+    def _():
+        arrived(rows.at[pl.ds(0, 2), :, others], s_row)
+        arrived(codes.at[pl.ds(0, 2), :, others], s_code)
 
     arrived(sq_own, s_sq)
-    arrived(rows.at[:, :, others], s_row)
-    arrived(codes.at[:, :, others], s_code)
     arrived(back.at[pl.ds(1, 2 * owners - 1)], s_back)
+
+
+def store_kernel(refined_ref, dist_ref, refined_out, dist_out, refined_sem, dist_sem):
+    copies = [
+        pltpu.make_async_copy(refined_ref, refined_out, refined_sem),
+        pltpu.make_async_copy(dist_ref, dist_out, dist_sem),
+    ]
+    for copy in copies:
+        copy.start()
+    for copy in copies:
+        copy.wait()
 
 
 def shards(vectors, list_ids, spill_weight, list_pos, old_centroids):
@@ -519,7 +562,7 @@
     cap = row_count * slot_count // (2 * owners)
     plane = owners // LINE
     fits = (
-        row_count == LANES and slot_count == 8 and owners * cap == LINE * LANES and plane & (plane - 1) == 0
+        row_count == LANES and slot_count == 8 and owners * cap == LINE * LANES and plane == 4
         and owners * slot_count == LANES and cap % 16 == 0 and lax.axis_size("rep") == 2
         and lists_here % LANES == 0 and feature_dim % (2 * LANES) == 0 and list_pos.shape[0] % LANES == 0
     )
@@ -548,6 +591,7 @@
             pltpu.VMEM((LINE, 2, meta_rows, 1, LANES), F32),
             pltpu.VMEM((slot_count, row_count), F32),
             pltpu.VMEM((LINE, 2, plane, cap, half), BF16),
+            pltpu.VMEM((2, 2, plane, cap, half), BF16),
             pltpu.VMEM((LINE, 2, plane, cap, half), BF16),
             pltpu.VMEM((LINE, 2, plane, 1, LANES), F32),
             pltpu.VMEM((LINE, 2 * LANES, lists_here), BF16),
@@ -561,10 +605,21 @@
             dma((4,)),
             dma((2,)), dma((2,)), dma((LINE, 2)), dma((LINE, 2)),
             dma(()), dma((LINE,)), dma(()), dma((LINE,)), dma(()), dma((LINE,)),
-            dma(()), dma(()), dma(()), dma(()),
+            dma(()), dma(()), dma(()), dma(()), dma(()), pltpu.SemaphoreType.REGULAR,
+            pltpu.SemaphoreType.REGULAR,
         ],
         compiler_params=pltpu.CompilerParams(collective_id=0, has_side_effects=True),
     )(vectors, list_ids.T, spill_weight.T, list_pos.reshape(-1, LANES), old_centroids)
+    refined, dist = pl.pallas_call(
+        store_kernel,
+        out_shape=(
+            pltpu.HBM((lists_here, feature_dim), F32),
+            pltpu.HBM((slot_count, row_count), F32),
+        ),
+        in_specs=[vmem, vmem],
+        out_specs=(hbm, hbm),
+        scratch_shapes=[dma(()), dma(())],
+    )(*(pltpu.with_memory_space_constraint(x, pltpu.MemorySpace.VMEM) for x in (refined, dist)))
     return refined, dist.T
 
 

time: 33.8 us -> 29.7 us (0.88)
  Pallas kernels: 31.3 us -> 28.9 us
  local copies, waits for them, and re-layouts: 1.74 us -> 0 us
    pallas_call x1, Pallas kernels: 31.3 us -> 27.8 us  [shards(): pl.pallas_call(functools.partial(line_kernel, owners, cap), out_shape=(pl...]
    unnamed x2 -> x0, local copies, waits for them, and re-layouts: 1.74 us -> none
    pallas_call x0 -> x1, Pallas kernels: none -> 1.16 us  [shards(): pl.pallas_call(store_kernel, out_shape=(pltpu.HBM((lists_here, feature_di...]
where the time goes in v3:
time: 29.7 us; the launch traced here: 29.6 us
  Pallas kernels  28.9 us (97%)
  between operations  0.64 us (2%)
    pallas_call x1, Pallas kernels, shards(): pl.pallas_call(functools.partial(line_kernel, owners, cap), out_shape=(pl...  27.8 us
    pallas_call x1, Pallas kernels, shards(): pl.pallas_call(store_kernel, out_shape=(pltpu.HBM((lists_here, feature_di...  1.16 us

profile of v3, /device:TPU:0, one launch (start us, length us, event | category | flops | bytes accessed | tf_op | source)
XLA Modules:
  0.0 29.6 jit_solution(5989211587858446448)
XLA Ops:
  0.6 27.8 %shard_map.68 = (f32[512,768]{1,0:T(8,128)S(1)}, f32[8,128]{1,0:T(8,128)S(1)}) custom-call(bf16[128,768]{1,0:T(8,128)(2,1)} %vec_hbm.1, s32[8,128]{1,0:T(8,128)} %bitcast.5, s32[8,128]{1,0:T(8,128)} %bitcast.6, s32[64,128]{1,0:T(8,128)} %bitcast.4, f32[512,768]{1,0:T(8,128)} %cent_hbm.1), custom_call_target="tpu_custom_call" | custom-call | tf_op jit(solution)/shard_map/pallas_call | solution.py:577
  28.4 1.2 %shard_map.69 = (f32[512,768]{1,0:T(8,128)}, f32[8,128]{1,0:T(8,128)}) custom-call(f32[512,768]{1,0:T(8,128)S(1)} %get-tuple-element.6.refined_ref, f32[8,128]{1,0:T(8,128)S(1)} %get-tuple-element.7.dist_ref), custom_call_target="tpu_custom_call" | custom-call | tf_op jit(solution)/shard_map/pallas_call | solution.py:613

commit v4 on v3

--- a/solution.py
+++ b/solution.py
@@ -145,6 +145,7 @@
 MESH = pl.DeviceIdType.MESH
 LANES = 128
 LINE = 4
+STORES = 1
 F32 = jnp.float32
 BF16 = jnp.bfloat16
 
@@ -181,7 +182,7 @@
     refined_ref, dist_ref,
     ints, vec_other, cent, cent_cat, raw_in, meta_in, seat_keep, send_buf, send_near, rows, codes,
     masks, placed, sq_own, sq_sib, acc, tot, back_send, back,
-    l_sem, s_own, s_meta, r_raw, r_meta, s_row, r_row, s_code, r_code, s_sq, r_sq, s_back, r_back, s_ref, r_ref, s_near, first, second,
+    l_sem, s_own, s_meta, r_half, r_raw, r_meta, s_row, r_row, s_code, r_code, s_sq, r_sq, s_back, r_back, s_ref, r_ref, s_near, first, second,
 ):
     me = lax.axis_index("grp")
     rep = lax.axis_index("rep")
@@ -246,20 +247,34 @@
     own_place = [z, near, inner]
     others = pl.ds(1, plane - 1)
 
+    own_half = row_count // 2
+
+    def row_half(ref, c):
+        return ref.at[pl.ds(c * own_half, own_half)]
+
     def own_raw(s, f):
         src = raw_in.at[0, 0] if f == 0 else vec_other
-        return remote(src, raw_in.at[s, f], s_own.at[s // 2], r_raw.at[s, f], own_place[s], 0, rep_of[f])
+        to = raw_in.at[s, f]
+        if s != 1:
+            return [remote(src, to, s_own.at[s // 2], r_raw.at[s, f], own_place[s], 0, rep_of[f])]
+        return [
+            remote(
+                row_half(src, c), row_half(to, c), s_own.at[0], r_half.at[f] if c == 0 else r_raw.at[1, f],
+                near, 0, rep_of[f],
+            )
+            for c in range(2)
+        ]
 
     def own_meta(s, f):
         return remote(
             meta_in.at[0, 0], meta_in.at[s, f], s_meta.at[s // 2], r_meta.at[s, f], own_place[s], 0, rep_of[f]
         )
 
-    def forward(f):
-        return (
-            remote(meta_in.at[1, f], meta_in.at[3, f], s_meta.at[1], r_meta.at[3, f], inner, 0, rep),
-            remote(raw_in.at[1, f], raw_in.at[3, f], s_own.at[1], r_raw.at[3, f], inner, 0, rep),
-        )
+    def forward(f, c):
+        if c is None:
+            return remote(meta_in.at[1, f], meta_in.at[3, f], s_meta.at[1], r_meta.at[3, f], inner, 0, rep)
+        src, to = row_half(raw_in.at[1, f], c), row_half(raw_in.at[3, f], c)
+        return remote(src, to, s_own.at[1], r_raw.at[3, f], inner, 0, rep)
 
     def row_copy(s, f, j):
         return remote(send_buf.at[s, f, j], rows.at[s, f, j], s_row, r_row.at[s], z, j, rep)
@@ -290,17 +305,20 @@
 
     pl.semaphore_wait(barrier, pbits + 3 + 2 * mid)
     def own_to(f):
-        own_raw(1, f).start()
+        for copy in own_raw(1, f):
+            copy.start()
 
         @pl.when(mid == 1)
         def _():
-            own_raw(2, f).start()
+            for copy in own_raw(2, f):
+                copy.start()
 
     tell(first, [1 << i for i in range(pbits)])
     local[0].wait()
     own_to(0)
     local[1].wait()
-    own_raw(0, 1).start()
+    for copy in own_raw(0, 1):
+        copy.start()
     pltpu.make_async_copy(ints, ints, l_sem.at[2]).wait()
     raw_ids = ints[pl.ds(0, slot_count)]
     weights = ints[pl.ds(slot_count, slot_count)]
@@ -372,28 +390,31 @@
             chosen = chosen + (meta_in[s, f, k] == q).astype(F32)
         return dot(chosen.astype(BF16), raw_in[s, f]).astype(BF16).reshape(plane, cap, half)
 
-    def pick(s, f):
-        to_near = s >= 2
+    def receive(s, f, passed_on=False):
+        arrived(meta_in.at[s, f], r_meta.at[s, f])
+        if passed_on:
+            forward(f, None).start()
+        if s == 1:
+            arrived(row_half(raw_in.at[1, f], 0), r_half.at[f])
+            if passed_on:
+                forward(f, 0).start()
+            arrived(row_half(raw_in.at[1, f], 1), r_raw.at[1, f])
+            if passed_on:
+                forward(f, 1).start()
+        else:
+            arrived(raw_in.at[s, f], r_raw.at[s, f])
+
+    def to_near(s, f):
+        for j in reversed(range(plane)):
+            near_code_copy(s, f, j).start()
+        send_near[s - 2, f] = picked_rows(s, f, s)
+        for j in reversed(range(plane)):
+            near_row_copy(s, f, j).start()
+
+    def to_plane(s, f):
         if (s, f) != (0, 0):
-            arrived(meta_in.at[s, f], r_meta.at[s, f])
-        for j in reversed(range(plane)):
-            if to_near:
-                near_code_copy(s, f, j).start()
-            if j and (s, f) != (0, 0):
+            for j in reversed(range(1, plane)):
                 code_copy(s, f, j).start()
-        if (s, f) != (0, 0):
-            arrived(raw_in.at[s, f], r_raw.at[s, f])
-        if to_near:
-            send_near[s - 2, f] = picked_rows(s, f, s)
-            for j in reversed(range(plane)):
-                near_row_copy(s, f, j).start()
-        elif s:
-
-            @pl.when(mid == 1)
-            def _():
-                for copy in forward(f):
-                    copy.start()
-
         picked = picked_rows(s, f, xz_of[s])
         send_buf[s, f] = picked
         if (s, f) == (0, 0):
@@ -404,11 +425,12 @@
         for j in reversed(range(1, plane)):
             row_copy(s, f, j).start()
         rows[s, f, 0] = picked[0]
+        codes[s, f, 0] = meta_in[s, f, slot_count + xz_of[s]]
 
     lane_row = iota((1, LANES), 1)
 
-    def code_row(s, f, picked_here=True):
-        out = meta_in[s, f, slot_count + xz_of[s]] if picked_here else codes[s, f, 0]
+    def code_row(s, f):
+        out = codes[s, f, 0]
         for j in range(1, plane):
             out = jnp.where(lane_row // cap == j, codes[s, f, j], out)
         return out
@@ -425,10 +447,16 @@
     def got_rows(s):
         return rows[s].reshape(2 * LANES, half).astype(F32)
 
+    centres = {}
+
     def near_part(s, picked_here=True):
+        before_rows(s, picked_here)
+        after_rows(s, picked_here)
+
+    def before_rows(s, picked_here=True):
         arrived(codes.at[s, :, others] if picked_here else codes.at[s], r_code.at[s])
         for f in range(2):
-            row = code_row(s, f, picked_here)
+            row = code_row(s, f)
             wide = to_col(row).astype(jnp.int32) // 8
             masks[s, pl.ds(f * LANES, LANES)] = (
                 (wide == iota((LANES, lists_here), 1)).astype(F32).astype(BF16)
@@ -436,15 +464,17 @@
             placed[s, :, pl.ds(f * LANES, LANES)] = (
                 (row.astype(jnp.int32) // 8 == iota((lists_here, LANES), 0)).astype(F32).astype(BF16)
             )
-        centre = halves(dot(masks[s], cent_cat[...]))
+        centres[s] = halves(dot(masks[s], cent_cat[...]))
+
+    def after_rows(s, picked_here=True):
         arrived(rows.at[s, :, others] if picked_here else rows.at[s], r_row.at[s])
-        diff = got_rows(s) - centre
+        diff = got_rows(s) - centres[s]
         sq_own[s] = lane_parts(diff * diff)
         sq_copy(s).start()
 
-    def far_part(s, picked_here=True):
+    def with_share_of(s):
         weight = jnp.concatenate(
-            [to_col((code_row(s, f, picked_here).astype(jnp.int32) % 8).astype(F32)) for f in range(2)], axis=0
+            [to_col((code_row(s, f).astype(jnp.int32) % 8).astype(F32)) for f in range(2)], axis=0
         )
         got = got_rows(s)
         sq_copy(s).wait_recv()
@@ -456,15 +486,20 @@
         added = dot(placed[s], jnp.concatenate([sv_hi, sv_lo, share_hi, share_lo], axis=1))
         sums = halves(added)
         counts = added[:, 2 * half : 2 * half + LANES] + added[:, 2 * half + LANES :]
-        acc[...] = (cent[...] if s == 0 else acc[...]) + sums
-        tot[...] = counts if s == 0 else tot[...] + counts
-
-    pick(0, 0)
+        if s == 0:
+            return cent[...] + sums, counts
+        return acc[...] + sums, tot[...] + counts
+
+    def far_part(s):
+        acc[...], tot[...] = with_share_of(s)
+
+    to_plane(0, 0)
     local[5].wait()
     hi, lo = split_two(cent[...])
     cent_cat[:, pl.ds(0, half)] = hi
     cent_cat[:, pl.ds(half, half)] = lo
-    pick(0, 1)
+    receive(0, 1)
+    to_plane(0, 1)
 
     def follow(steps):
         for step, args in steps:
@@ -474,21 +509,24 @@
     def _():
         pl.semaphore_wait(second, 1)
         follow([
-            (pick, (1, 0)), (pick, (2, 0)), (pick, (1, 1)), (pick, (2, 1)), (near_part, (0,)), (pick, (3, 0)), (pick, (3, 1)),
+            (receive, (1, 0, True)), (receive, (2, 0)), (to_near, (2, 0)), (receive, (1, 1, True)), (receive, (2, 1)), (to_near, (2, 1)),
+            (to_plane, (1, 0)), (to_plane, (2, 0)), (to_plane, (1, 1)), (to_plane, (2, 1)), (near_part, (0,)),
+            (receive, (3, 0)), (to_near, (3, 0)), (to_plane, (3, 0)), (receive, (3, 1)), (to_near, (3, 1)), (to_plane, (3, 1)),
             (far_part, (0,)), (near_part, (1,)), (near_part, (2,)), (far_part, (1,)), (near_part, (3,)), (far_part, (2,)),
-            (far_part, (3,)),
         ])
 
     @pl.when(mid == 0)
     def _():
         pl.semaphore_wait(second, 1)
         follow([
-            (pick, (1, 0)), (pick, (1, 1)), (near_part, (0,)), (near_part, (1,)), (far_part, (0,)), (far_part, (1,)),
-            (near_part, (2, False)), (near_part, (3, False)), (far_part, (2, False)), (far_part, (3, False)),
+            (receive, (1, 0)), (to_plane, (1, 0)), (receive, (1, 1)), (to_plane, (1, 1)), (near_part, (0,)), (near_part, (1,)),
+            (far_part, (0,)), (far_part, (1,)),
+            (near_part, (2, False)), (before_rows, (3, False)), (far_part, (2,)), (after_rows, (3, False)),
         ])
 
-    scale = 1.0 / (1.0 + tot[...])
-    refined = acc[...] * jnp.concatenate([scale] * (half // LANES), axis=1)
+    sums, counts = with_share_of(LINE - 1)
+    scale = 1.0 / (1.0 + counts)
+    refined = sums * jnp.concatenate([scale] * (half // LANES), axis=1)
     refined_ref[:, mine] = refined
     hi, lo = split_two(refined)
     cent_cat[:, pl.ds(0, half)] = hi
@@ -500,7 +538,7 @@
         for f in range(2):
             row = to_row(value[f * LANES : (f + 1) * LANES])
             back_send[s, f] = row
-            for j in range(plane):
+            for j in reversed(range(plane)):
                 if (s, f, j) != (0, 0, 0):
                     back_copy(s, f, j).start()
             if (s, f) == (0, 0):
@@ -543,11 +581,12 @@
     arrived(back.at[pl.ds(1, 2 * owners - 1)], s_back)
 
 
-def store_kernel(refined_ref, dist_ref, refined_out, dist_out, refined_sem, dist_sem):
-    copies = [
-        pltpu.make_async_copy(refined_ref, refined_out, refined_sem),
-        pltpu.make_async_copy(dist_ref, dist_out, dist_sem),
-    ]
+def store_kernel(refined_ref, dist_ref, refined_out, dist_out, sems):
+    part = refined_ref.shape[0] // STORES
+    copies = [pltpu.make_async_copy(dist_ref, dist_out, sems.at[STORES])]
+    for i in range(STORES):
+        span = pl.ds(i * part, part)
+        copies.append(pltpu.make_async_copy(refined_ref.at[span], refined_out.at[span], sems.at[i]))
     for copy in copies:
         copy.start()
     for copy in copies:
@@ -603,7 +642,7 @@
             pltpu.VMEM((LINE, 2, 1, LANES), F32),
             pltpu.VMEM((2 * owners, 1, LANES), F32),
             dma((4,)),
-            dma((2,)), dma((2,)), dma((LINE, 2)), dma((LINE, 2)),
+            dma((2,)), dma((2,)), dma((2,)), dma((LINE, 2)), dma((LINE, 2)),
             dma(()), dma((LINE,)), dma(()), dma((LINE,)), dma(()), dma((LINE,)),
             dma(()), dma(()), dma(()), dma(()), dma(()), pltpu.SemaphoreType.REGULAR,
             pltpu.SemaphoreType.REGULAR,
@@ -618,7 +657,7 @@
         ),
         in_specs=[vmem, vmem],
         out_specs=(hbm, hbm),
-        scratch_shapes=[dma(()), dma(())],
+        scratch_shapes=[dma((STORES + 1,))],
     )(*(pltpu.with_memory_space_constraint(x, pltpu.MemorySpace.VMEM) for x in (refined, dist)))
     return refined, dist.T
 

time: 29.7 us -> 29.8 us (level)
  no operation moved by 1% of the time
where the time goes in v4:
time: 29.8 us; the launch traced here: 29.7 us
  Pallas kernels  29 us (97%)
  between operations  0.64 us (2%)
    pallas_call x1, Pallas kernels, shards(): pl.pallas_call(functools.partial(line_kernel, owners, cap), out_shape=(pl...  27.9 us
    pallas_call x1, Pallas kernels, shards(): pl.pallas_call(store_kernel, out_shape=(pltpu.HBM((lists_here, feature_di...  1.17 us

profile of v4, /device:TPU:0, one launch (start us, length us, event | category | flops | bytes accessed | tf_op | source)
XLA Modules:
  0.0 29.7 jit_solution(4666686338257438721)
XLA Ops:
  0.6 27.9 %shard_map.68 = (f32[512,768]{1,0:T(8,128)S(1)}, f32[8,128]{1,0:T(8,128)S(1)}) custom-call(bf16[128,768]{1,0:T(8,128)(2,1)} %vec_hbm.1, s32[8,128]{1,0:T(8,128)} %bitcast.5, s32[8,128]{1,0:T(8,128)} %bitcast.6, s32[64,128]{1,0:T(8,128)} %bitcast.4, f32[512,768]{1,0:T(8,128)} %cent_hbm.1), custom_call_target="tpu_custom_call" | custom-call | tf_op jit(solution)/shard_map/pallas_call | solution.py:616
  28.5 1.2 %shard_map.69 = (f32[512,768]{1,0:T(8,128)}, f32[8,128]{1,0:T(8,128)}) custom-call(f32[512,768]{1,0:T(8,128)S(1)} %get-tuple-element.6.refined_ref, f32[8,128]{1,0:T(8,128)S(1)} %get-tuple-element.7.dist_ref), custom_call_target="tpu_custom_call" | custom-call | tf_op jit(solution)/shard_map/pallas_call | solution.py:652
